TPU v7x, 32 devices: a whole 2x2x4 slice. The times are simulated.
32 devices in a mesh: dp: 8 (over z, x), cand: 4 (over y, core).
Axes of the slice: x: 2, y: 2, z: 4, core: 2. Of those that a mesh axis runs over, the one named last changes fastest.
Arguments:
- hidden: bfloat16 [16, 32, 128, 768], P('dp', 'cand'), may hold values from -24 to 24
- attn_weight: bfloat16 [768, 3072], P('dp'), may hold values from -1 to 1
- norm_gain: float32 [768], replicated, may hold values from 0.2 to 4
- pos_bias: float32 [12, 128, 128], replicated, may hold values from -5 to 5
- score_weight: float32 [768], replicated, may hold values from -4 to 4
- pair_lengths: int32 [16, 32], P('dp', 'cand'), may hold values from 32 to 128
- labels: int32 [16, 32], P('dp', 'cand'), may hold values from 0 to 3
Outputs:
- update: float32 [768, 3072], P('dp')
- loss: float32 [16], P('dp')
All inputs are finite; a program needn't handle non-finite values.
Results may differ from a plain program's by a relative error of at most 0.017.
Values may be sent and summed in bfloat16 or wider, within the bound.
No kernel may reach another device: no remote copies, remote signals or barrier semaphores. Data moves between devices by JAX's collectives and lax.ppermute only.
A program may use at most 128 MiB of HBM per device.

v0:
```python
import jax
import jax.numpy as jnp
from jax import lax
from jax.sharding import PartitionSpec as P

EPS = 1e-06


def rms_rows(values, gain):
    factor = lax.rsqrt(jnp.mean(values * values, axis=-1, keepdims=True) + EPS)
    return values * factor * gain


def attend(qkv, pos_bias, pair_len):
    batch, seq, triple = qkv.shape
    width = triple // 3
    heads = pos_bias.shape[0]
    head_size = width // heads
    parts = qkv.reshape(batch, seq, 3, heads, head_size)
    logits = jnp.einsum(
        "bqhd,bkhd->bhqk", parts[:, :, 0], parts[:, :, 1], preferred_element_type=jnp.float32
    )
    logits = logits + pos_bias[None]
    valid = jnp.arange(seq, dtype=jnp.int32)[None, :] < pair_len[:, None]
    logits = jnp.where(valid[:, None, None, :], logits, -1e30)
    highest = jnp.max(logits, axis=-1, keepdims=True)
    expo = jnp.exp(logits - highest)
    probs = (expo / jnp.sum(expo, axis=-1, keepdims=True)).astype(jnp.bfloat16)
    context = jnp.einsum(
        "bhqk,bkhd->bqhd", probs, parts[:, :, 2], preferred_element_type=jnp.float32
    )
    return context.astype(jnp.bfloat16).reshape(batch, seq, width)


def score_head(pooled, score_weight):
    return jnp.sum(rms_rows(pooled, 1.0) * score_weight, axis=-1)


def shards(hidden, attn_weight, norm_gain, pos_bias, score_weight, pair_lengths, labels):
    q_local, c_local, seq, width = hidden.shape
    weights = lax.all_gather(attn_weight, "dp", axis=0, tiled=True)
    tokens = hidden.reshape(q_local * c_local, seq, width)
    pair_len = pair_lengths.reshape(-1)
    values = tokens.astype(jnp.float32)
    normed = rms_rows(values, norm_gain).astype(jnp.bfloat16)
    flat_norm = normed.reshape(-1, width)
    qkv = jnp.dot(flat_norm, weights[:, : 3 * width], preferred_element_type=jnp.float32)
    qkv = qkv.astype(jnp.bfloat16).reshape(q_local * c_local, seq, 3 * width)
    context, attend_back = jax.vjp(lambda block: attend(block, pos_bias, pair_len), qkv)
    flat_ctx = context.reshape(-1, width)
    out_rows = values + jnp.dot(
        flat_ctx, weights[:, 3 * width :], preferred_element_type=jnp.float32
    ).reshape(values.shape)
    live = (jnp.arange(seq, dtype=jnp.int32)[None, :] < pair_len[:, None]).astype(jnp.float32)
    share = live / pair_len.astype(jnp.float32)[:, None]
    pooled = jnp.sum(out_rows * share[:, :, None], axis=1)
    flat_scores, head_back = jax.vjp(lambda vector: score_head(vector, score_weight), pooled)
    scores = flat_scores.reshape(q_local, c_local)
    target = jnp.exp(labels.astype(jnp.float32))
    highest = lax.pmax(jnp.max(scores, axis=1), "cand")
    expsum, target_sum, target_dot = lax.psum(
        (
            jnp.sum(jnp.exp(scores - highest[:, None]), axis=1),
            jnp.sum(target, axis=1),
            jnp.sum(target * scores, axis=1),
        ),
        "cand",
    )
    loss = highest + jnp.log(expsum) - target_dot / target_sum
    score_grad = jnp.exp(scores - highest[:, None]) / expsum[:, None] - target / target_sum[:, None]
    pooled_grad = head_back(score_grad.reshape(-1))[0]
    out_grad = (pooled_grad[:, None, :] * share[:, :, None]).astype(jnp.bfloat16)
    flat_out = out_grad.reshape(-1, width)
    context_grad = jnp.dot(flat_out, weights[:, 3 * width :].T, preferred_element_type=jnp.float32)
    context_grad = context_grad.astype(jnp.bfloat16).reshape(context.shape)
    qkv_grad = attend_back(context_grad)[0].reshape(-1, 3 * width)
    dims = (((0,), (0,)), ((), ()))
    first = lax.dot_general(flat_norm, qkv_grad, dims, preferred_element_type=jnp.float32)
    second = lax.dot_general(flat_ctx, flat_out, dims, preferred_element_type=jnp.float32)
    shard = lax.psum_scatter(
        jnp.concatenate([first, second], axis=1).astype(jnp.bfloat16),
        "dp",
        scatter_dimension=0,
        tiled=True,
    ).astype(jnp.float32)
    shard = lax.psum(shard.astype(jnp.bfloat16), "cand").astype(jnp.float32)
    squares = lax.psum(jnp.sum(shard * shard), "dp")
    rms_value = jnp.sqrt(squares / (4.0 * width * width))
    update = shard / (rms_value + EPS)
    return (update, loss)


def solution(mesh):
    in_specs = (
        P("dp", "cand", None, None),
        P("dp", None),
        P(),
        P(),
        P(),
        P("dp", "cand"),
        P("dp", "cand"),
    )
    out_specs = (P("dp", None), P("dp"))
    return jax.shard_map(shards, mesh=mesh, in_specs=in_specs, out_specs=out_specs, check_vma=False)
```

profile of v0, /device:TPU:0, one launch (start us, length us, event | category | flops | bytes accessed | tf_op | source)
XLA Modules:
  0.0 460.7 jit_solution(10536083495842605806)
XLA Ops:
  11.3 2.6 multiply_reduce_fusion
  13.9 2.5 multiply_convert_fusion.1
  16.4 2.4 fusion.13
  18.8 73.4 %all-gather.2.cloned.1.call-done = bf16[768,3072]{1,0:T(8,128)(2,1)} async-done(((bf16[96,3072]{1,0:T(8,128)(2,1)}), bf16[768,3072]{1,0:T(8,128)(2,1)}) %all-gather.2.cloned.1.call-update) | async-done | bytes 4718608 | tf_op jit(solution)/shard_map/all_gather | solution.py:41
  92.3 12.5 %convolution_convert_fusion = bf16[2048,2304]{1,0:T(8,128)(2,1)} fusion(bf16[2048,768]{1,0:T(8,128)(2,1)} %fusion.13, bf16[768,3072]{1,0:T(8,128)(2,1)} %all-gather.2.cloned.1.call-done), kind=kOutput, calls=%fused_computation.11 | convolution fusion | flops 7252475904 | bytes 16121856 | tf_op jit(solution)/shard_map/dot_general | solution.py:47
  104.8 12.7 %copy.20 = bf16[2048,2304]{0,1:T(8,128)(2,1)} copy(bf16[2048,2304]{1,0:T(8,128)(2,1)} %convolution_convert_fusion) | data formatting | bytes 18874368 | tf_op jit(solution)/shard_map/convert_element_type | solution.py:48
  117.5 10.9 %copy.45 = bf16[288,8,16,128]{3,2,1,0:T(8,128)(2,1)} copy(bf16[288,8,16,128]{3,1,2,0:T(8,128)(2,1)} %bitcast.104) | data formatting | bytes 18874368
  128.4 6.4 %fusion.56 = (bf16[16,128,1,12,64]{1,0,4,3,2:T(8,128)(2,1)}, bf16[16,128,1,12,64]{1,0,4,3,2:T(8,128)(2,1)}, bf16[16,128,1,12,64]{1,0,4,3,2:T(8,128)(2,1)S(1)}) fusion(bf16[16,128,3,12,64]{1,0,4,3,2:T(8,128)(2,1)} %bitcast.103), kind=kLoop, calls=%fused_computation.91 | loop fusion | bytes 18874368 | tf_op jit(solution)/shard_map/jvp()/slice | solution.py:30
  134.8 7.5 %fusion.5 = (f32[16,12,128]{2,1,0:T(8,128)S(1)}, f32[16,12,128,128]{2,3,1,0:T(8,128)S(1)}) fusion(f32[12,128,128]{1,2,0:T(8,128)S(1)} %copy-done.11, pred[16,128]{1,0:T(8,128)(4,1)S(1)} %iota_compare_fusion, bf16[16,128,1,12,64]{1,0,4,3,2:T(8,128)(2,1)S(1)} %get-tuple-element.15, bf16[16,128,1,12,64]{1,0,4,3,2:T(8,128)(2,1)} %get-tuple-element.14), kind=kOutput, calls=%fused_computation.13 | convolution fusion | flops 412065792 | bytes 19761152 | tf_op jit(solution)/shard_map/jvp(bqhd,bkhd->bhqk)/dot_general | solution.py:20
  142.3 3.4 fusion.37
  146.9 8.1 %convert_reduce_fusion = (f32[16,12,128]{2,1,0:T(8,128)S(1)}, pred[16,12,128,128]{2,3,1,0:T(32,128)(4,1)}, bf16[16,12,128,128]{2,3,1,0:T(8,128)(2,1)S(1)}) fusion(f32[16,12,128]{2,1,0:T(8,128)S(1)} %get-tuple-element.20, f32[16,12,128,128]{2,3,1,0:T(8,128)S(1)} %get-tuple-element.21, f32[12,128,128]{1,2,0:T(8,128)S(1)} %copy-done.11, ...), kind=kLoop, calls=%fused_computation.7 | loop fusion | flops 25141248 | bytes 23103488 | tf_op jit(solution)/shard_map/jvp()/reduce_sum | solution.py:26
  155.0 2.7 fusion.36
  159.2 4.6 fusion.15
  164.3 5.7 %pmax.7 = f32[2]{0:T(128)S(1)} all-reduce(f32[2]{0:T(128)S(1)} %reduce_max.19), channel_id=1, replica_groups=mesh['dp'=8,'cand'=4] {'cand'}, use_global_device_ids=true, to_apply=%region_7.8 | all-reduce | flops 2 | bytes 16 | tf_op jit(solution)/shard_map/pmax | solution.py:60
  170.2 6.6 %all-reduce.3 = (f32[2]{0:T(128)S(1)}, f32[2]{0:T(128)S(1)}, f32[2]{0:T(128)S(1)}) all-reduce(f32[2]{0:T(128)S(1)} %get-tuple-element.3, f32[2]{0:T(128)S(1)} %get-tuple-element.4, f32[2]{0:T(128)S(1)} %get-tuple-element.2), channel_id=1, replica_groups=mesh['dp'=8,'cand'=4] {'cand'}, use_global_device_ids=true, to_apply=%region_11.12 | all-reduce | flops 6 | bytes 48 | tf_op jit(solution)/shard_map/psum | solution.py:61
  177.7 5.3 %convolution_convert_fusion.2 = bf16[2048,768]{1,0:T(8,128)(2,1)} fusion(bf16[2048,768]{1,0:T(8,128)(2,1)S(1)} %fusion.11, bf16[768,3072]{1,0:T(8,128)(2,1)} %all-gather.2.cloned.1.call-done), kind=kOutput, calls=%fused_computation.41 | convolution fusion | flops 2417491968 | bytes 7471104 | tf_op jit(solution)/shard_map/dot_general | solution.py:74
  182.9 4.7 %copy.27 = bf16[2048,768]{0,1:T(8,128)(2,1)} copy(bf16[2048,768]{1,0:T(8,128)(2,1)} %convolution_convert_fusion.2) | data formatting | bytes 6291456 | tf_op jit(solution)/shard_map/convert_element_type | solution.py:75
  187.7 2.9 copy.46
  192.2 9.0 %convert_bitcast_fusion.2 = bf16[16,128,1,12,64]{1,4,3,0,2:T(8,128)(2,1)} fusion(bf16[16,12,128,128]{2,3,1,0:T(8,128)(2,1)} %copy-done.2, bf16[16,12,64,128]{3,0,2,1:T(8,128)(2,1)S(1)} %bitcast.108), kind=kOutput, calls=%fused_computation.50 | convolution fusion | flops 404226048 | bytes 12582912 | tf_op jit(solution)/shard_map/transpose(jvp(bhqk,bkhd->bqhd))/dot_general | solution.py:29
  201.2 12.6 %fusion.3 = (f32[16,12,128]{2,1,0:T(8,128)S(1)}, bf16[16,12,128,128]{2,3,1,0:T(8,128)(2,1)}) fusion(f32[16,12,128]{2,1,0:T(8,128)S(1)} %multiply_divide_fusion, f32[16,12,128]{2,1,0:T(8,128)S(1)} %get-tuple-element.20, f32[16,12,128,128]{2,3,1,0:T(8,128)} %copy-done, f32[12,128,128]{1,2,0:T(8,128)S(1)} %copy-done.11, ...), kind=kOutput, calls=%fused_computation.5 | convolution fusion | flops 427794432 | bytes 26249216 | tf_op jit(solution)/shard_map/transpose(jvp(bhqk,bkhd->bqhd))/dot_general | solution.py:29
  213.9 10.1 %fusion.53 = (f32[16,12,128]{2,1,0:T(8,128)S(1)}, f32[16,12,128,128]{2,3,1,0:T(8,128)}) fusion(f32[16,12,128]{2,1,0:T(8,128)S(1)} %get-tuple-element.20, f32[16,12,128,128]{2,3,1,0:T(8,128)S(1)} %bitcast.102, f32[12,128,128]{1,2,0:T(8,128)S(1)} %copy-done.11, pred[16,128]{1,0:T(8,128)(4,1)S(1)} %iota_compare_fusion, f32[16,12,128]{2,1,0:T(8,128)S(1)} %neg.9, ...), kind=kLoop, calls=%fused_computation.90 | loop fusion | flops 25141248 | bytes 32638976 | tf_op jit(solution)/shard_map/transpose(jvp())/reduce_sum | solution.py:27
  224.1 11.4 %convert_bitcast_fusion.1 = bf16[16,128,1,12,64]{1,4,3,0,2:T(8,128)(2,1)} fusion(bf16[16,128,1,12,64]{1,0,4,3,2:T(8,128)(2,1)} %get-tuple-element.14, f32[16,12,128,128]{2,3,1,0:T(8,128)} %get-tuple-element.9, pred[16,12,128,128]{2,3,1,0:T(32,128)(4,1)} %get-tuple-element.11, f32[16,12,128]{2,1,0:T(8,128)S(1)} %negate_divide_fusion, ...), kind=kOutput, calls=%fused_computation.49 | convolution fusion | flops 413663232 | bytes 22120448 | tf_op jit(solution)/shard_map/transpose(jvp(bqhd,bkhd->bhqk))/dot_general | solution.py:20
  237.0 4.2 convert_bitcast_fusion
  244.2 6.8 %pad_add_fusion = bf16[16,128,3,12,64]{1,4,3,0,2:T(8,128)(2,1)} fusion(bf16[16,128,1,12,64]{1,4,3,0,2:T(8,128)(2,1)} %convert_bitcast_fusion, bf16[16,128,1,12,64]{1,4,3,0,2:T(8,128)(2,1)} %convert_bitcast_fusion.1, bf16[16,128,1,12,64]{1,4,3,0,2:T(8,128)(2,1)S(1)} %copy-done.12), kind=kLoop, calls=%fused_computation.17 | loop fusion | flops 9437184 | bytes 18874368 | tf_op jit(solution)/shard_map/transpose(jvp())/add_any | solution.py:21
  251.0 26.1 %copy.33 = bf16[16,128,3,12,64]{1,0,4,3,2:T(8,128)(2,1)} copy(bf16[16,128,3,12,64]{1,4,3,0,2:T(8,128)(2,1)} %pad_add_fusion) | data formatting | bytes 18874368 | tf_op jit(solution)/shard_map/transpose(jvp())/add_any | solution.py:21
  277.2 2.4 copy.34
  279.6 11.4 %fusion.22 = bf16[768,2304]{1,0:T(8,128)(2,1)S(1)} fusion(bf16[2048,768]{1,0:T(8,128)(2,1)S(1)} %bitcast.113, bf16[288,8,16,128]{3,2,1,0:T(8,128)(2,1)} %bitcast.110), kind=kOutput, calls=%fused_computation.37 | convolution fusion | flops 7249526784 | bytes 16121856 | tf_op jit(solution)/shard_map/dot_general | solution.py:78
  291.0 2.6 fusion.38
  293.7 2.8 pad_maximum_fusion
  296.5 94.1 %reduce-scatter.2.cloned.1.call-done = bf16[96,3072]{1,0:T(8,128)(2,1)} async-done(((bf16[768,3072]{1,0:T(8,128)(2,1)}), bf16[96,3072]{1,0:T(8,128)(2,1)}) %reduce-scatter.2.cloned.1.call-update) | async-done | bytes 589840 | tf_op jit(solution)/shard_map/reduce_scatter | solution.py:80
  390.6 35.8 %all-reduce.6.cloned.1.call-done = bf16[96,3072]{1,0:T(8,128)(2,1)} async-done(((bf16[96,3072]{1,0:T(8,128)(2,1)}), bf16[96,3072]{1,0:T(8,128)(2,1)}) %all-reduce.6.cloned.1.call-update) | async-done | bytes 589840 | tf_op jit(solution)/shard_map/psum | solution.py:86
  428.9 22.0 %psum.38 = f32[]{:T(128)} all-reduce(f32[]{:T(128)} %fusion.41), channel_id=1, replica_groups=mesh['dp'=8,'cand'=4] {'dp'}, use_global_device_ids=true, to_apply=%region_19.20 | all-reduce | flops 1 | bytes 8 | tf_op jit(solution)/shard_map/psum | solution.py:87
  (76 shorter events, 19.3 us)
Async XLA Ops:
  7.2 6.8 %copy-start.5 = (bf16[2,8,128,768]{3,2,1,0:T(8,128)(2,1)S(1)}, bf16[2,8,128,768]{3,2,1,0:T(8,128)(2,1)}, u32[]{:S(2)}) copy-start(bf16[2,8,128,768]{3,2,1,0:T(8,128)(2,1)} %param.7) | copy-start | bytes 9437188
  7.2 6.8 %copy-start.17 = (f32[768]{0:T(1024)S(1)}, f32[768]{0:T(1024)}, u32[]{:S(2)}) copy-start(f32[768]{0:T(1024)} %param.9) | copy-start | bytes 9220
  7.2 85.1 %all-gather.2.cloned.1.call-start = ((), (), s32[]{:S(2)}) async-start(), calls=%async_computation.1 | async-start | bytes 5308416 | tf_op jit(solution)/shard_map/all_gather | solution.py:41
  7.9 382.7 %reduce-scatter.2.cloned.1.call-start = ((), (), s32[]{:S(2)}) async-start(), calls=%async_computation.2 | async-start | bytes 5308416 | tf_op jit(solution)/shard_map/reduce_scatter | solution.py:80
  128.4 6.4 %copy-start.11 = (f32[12,128,128]{1,2,0:T(8,128)S(1)}, f32[12,128,128]{1,2,0:T(8,128)}, u32[]{:S(2)}) copy-start(f32[12,128,128]{1,2,0:T(8,128)} %copy.24) | copy-start | bytes 2359300
  134.8 7.6 %copy-start.3 = (bf16[16,128,1,12,64]{1,0,4,3,2:T(8,128)(2,1)}, bf16[16,128,1,12,64]{1,0,4,3,2:T(8,128)(2,1)S(1)}, u32[]{:S(2)}) copy-start(bf16[16,128,1,12,64]{1,0,4,3,2:T(8,128)(2,1)S(1)} %get-tuple-element.15) | copy-start | bytes 9437188
  142.3 4.6 copy-start
  146.9 8.1 %copy-start.8 = (bf16[16,128,1,12,64]{1,0,4,3,2:T(8,128)(2,1)S(1)}, bf16[16,128,1,12,64]{1,0,4,3,2:T(8,128)(2,1)}, u32[]{:S(2)}) copy-start(bf16[16,128,1,12,64]{1,0,4,3,2:T(8,128)(2,1)} %get-tuple-element.13) | copy-start | bytes 9437188
  155.0 3.2 copy-start.2
  155.0 4.2 copy-start.6
  158.2 5.6 %copy-start.9 = (bf16[16,12,64,128]{3,2,1,0:T(8,128)(2,1)}, bf16[16,12,64,128]{3,2,1,0:T(8,128)(2,1)S(1)}, u32[]{:S(2)}) copy-start(bf16[16,12,64,128]{3,2,1,0:T(8,128)(2,1)S(1)} %fusion.36) | copy-start | bytes 9437188
  159.2 4.7 %copy-start.16 = (f32[768]{0:T(1024)S(1)}, f32[768]{0:T(1024)}, u32[]{:S(2)}) copy-start(f32[768]{0:T(1024)} %param.11) | copy-start | bytes 9220
  159.2 10.8 %copy-start.18 = (s32[2,8]{1,0:T(2,128)S(1)}, s32[2,8]{1,0:T(2,128)}, u32[]{:S(2)}) copy-start(s32[2,8]{1,0:T(2,128)} %param.13) | copy-start | bytes 196
  190.5 1.6 copy-start.13
  192.2 21.7 %slice-start = ((s8[12582912]{0:T(1024)(128)(4,1)}), s8[4194304]{0:T(1024)(128)(4,1)S(1)}, s32[]{:S(2)}) async-start(s8[12582912]{0:T(1024)(128)(4,1)} %bitcast.101), calls=%async_computation.4 | async-start | bytes 8388608
  201.2 12.7 %slice-start.1 = ((s8[12582912]{0:T(1024)(128)(4,1)}), s8[4194304]{0:T(1024)(128)(4,1)S(1)}, s32[]{:S(2)}) async-start(s8[12582912]{0:T(1024)(128)(4,1)} %bitcast.101), calls=%async_computation.5 | async-start | bytes 8388608
  201.2 12.7 %slice-start.2 = ((s8[12582912]{0:T(1024)(128)(4,1)}), s8[4194304]{0:T(1024)(128)(4,1)S(1)}, s32[]{:S(2)}) async-start(s8[12582912]{0:T(1024)(128)(4,1)} %bitcast.101), calls=%async_computation.6 | async-start | bytes 8388608
  224.1 11.4 %copy-start.1 = (f32[16,12,128,128]{2,3,1,0:T(8,128)S(1)}, f32[16,12,128,128]{2,3,1,0:T(8,128)}, u32[]{:S(2)}) copy-start(f32[16,12,128,128]{2,3,1,0:T(8,128)} %get-tuple-element.9) | copy-start | bytes 37748740
  224.1 11.8 %copy-start.4 = (bf16[16,128,1,12,64]{1,0,4,3,2:T(8,128)(2,1)S(1)}, bf16[16,128,1,12,64]{1,0,4,3,2:T(8,128)(2,1)}, u32[]{:S(2)}) copy-start(bf16[16,128,1,12,64]{1,0,4,3,2:T(8,128)(2,1)} %copy-done.3) | copy-start | bytes 9437188
  224.1 12.9 %copy-start.7 = (pred[16,12,128,128]{2,3,1,0:T(32,128)(4,1)S(1)}, pred[16,12,128,128]{2,3,1,0:T(32,128)(4,1)}, u32[]{:S(2)}) copy-start(pred[16,12,128,128]{2,3,1,0:T(32,128)(4,1)} %get-tuple-element.11) | copy-start | bytes 9437188
  241.2 3.0 copy-start.12
  251.0 26.2 %copy-start.10 = (bf16[16,12,64,128]{3,2,1,0:T(8,128)(2,1)S(1)}, bf16[16,12,64,128]{3,2,1,0:T(8,128)(2,1)}, u32[]{:S(2)}) copy-start(bf16[16,12,64,128]{3,2,1,0:T(8,128)(2,1)} %copy-done.9) | copy-start | bytes 9437188
  277.2 2.5 copy-start.15
  279.6 11.4 %copy-start.14 = (bf16[16,128,768]{2,1,0:T(8,128)(2,1)S(1)}, bf16[16,128,768]{2,1,0:T(8,128)(2,1)}, u32[]{:S(2)}) copy-start(bf16[16,128,768]{2,1,0:T(8,128)(2,1)} %multiply_convert_fusion) | copy-start | bytes 9437188
  296.5 130.0 %all-reduce.6.cloned.1.call-start = ((), (), s32[]{:S(2)}) async-start(), calls=%async_computation.3 | async-start | bytes 1179648 | tf_op jit(solution)/shard_map/psum | solution.py:86
Sparse Core Ops, SparseCore 0:
  10.2 82.0 all-gather.1
  296.6 93.9 reduce-scatter.1
  393.0 33.3 all-reduce.5
where the time goes:
time: 464 us; the launch traced here: 461 us
  waiting for transfers between devices  204 us (44%)
  matrix products  83.9 us (18%)
  local copies, waits for them, and re-layouts  76.2 us (16%)
  other arithmetic  47.1 us (10%)
  blocking collectives  34.2 us (7%)
  between operations  15.2 us (3%)
    reduce_scatter x1, waiting for transfers between devices, shards(): lax.psum_scatter(jnp.concatenate([first, second], axis=1).astype(jnp.bflo...  94.1 us
    all_gather x1, waiting for transfers between devices, shards(): weights = lax.all_gather(attn_weight, 'dp', axis=0, tiled=True)  73.4 us
    psum x1, waiting for transfers between devices, shards(): shard = lax.psum(shard.astype(jnp.bfloat16), 'cand').astype(jnp.float32)  35.8 us
    add_any x1, local copies, waits for them, and re-layouts, attend(): parts[:, :, 0]  26.1 us
    dot_general x3, matrix products, attend(): jnp.einsum('bhqk,bkhd->bqhd', probs, parts[:, :, 2], preferred_element_ty...  24.4 us
    dot_general x3, matrix products, attend(): jnp.einsum('bqhd,bkhd->bhqk', parts[:, :, 0], parts[:, :, 1], preferred_e...  23.1 us
    unnamed x47, local copies, waits for them, and re-layouts  22.7 us
    psum x1, blocking collectives, shards(): squares = lax.psum(jnp.sum(shard * shard), 'dp')  22 us
  transfers between devices with their start and end apart: 3, of which 3 were waited for; matrix products, arithmetic and copies ran while one was open for 2% of the time, Pallas kernels for 0%

commit v1 on v0

--- a/solution.py
+++ b/solution.py
@@ -38,7 +38,12 @@
 
 def shards(hidden, attn_weight, norm_gain, pos_bias, score_weight, pair_lengths, labels):
     q_local, c_local, seq, width = hidden.shape
-    weights = lax.all_gather(attn_weight, "dp", axis=0, tiled=True)
+    ring = [attn_weight]
+    for hop in range(7):
+        ring.append(lax.ppermute(ring[-1], "dp", [(dev, (dev + 1) % 8) for dev in range(8)]))
+    weights = jnp.roll(
+        jnp.concatenate(ring[::-1], axis=0), (lax.axis_index("dp") + 1) * ring[0].shape[0], axis=0
+    )
     tokens = hidden.reshape(q_local * c_local, seq, width)
     pair_len = pair_lengths.reshape(-1)
     values = tokens.astype(jnp.float32)

time: 464 us -> 501 us (1.080)
  waiting for transfers between devices: 204 us -> 227 us
  local copies, waits for them, and re-layouts: 76.2 us -> 87.5 us
    ppermute x0 -> x7, waiting for transfers between devices: none -> 98.1 us  [shards(): lax.ppermute(ring[-1], 'dp', [(dev, (dev + 1) % 8) for dev in range(8)])]
    all_gather x1 -> x0, waiting for transfers between devices: 73.4 us -> none  [shards(): weights = lax.all_gather(attn_weight, 'dp', axis=0, tiled=True)]
    unnamed x47 -> x72, local copies, waits for them, and re-layouts: 22.7 us -> 34.1 us
  transfers between devices with their start and end apart: 3 -> 9, of which waited for: 3 -> 9; matrix products, arithmetic and copies ran while one was open for 2% -> 2% of each run, Pallas kernels for 0% -> 0%
where the time goes in v1:
time: 501 us; the launch traced here: 496 us
  waiting for transfers between devices  227 us (45%)
  local copies, waits for them, and re-layouts  87.5 us (17%)
  matrix products  81.9 us (16%)
  other arithmetic  47.5 us (9%)
  blocking collectives  33.5 us (7%)
  between operations  15.6 us (3%)
    ppermute x7, waiting for transfers between devices, shards(): lax.ppermute(ring[-1], 'dp', [(dev, (dev + 1) % 8) for dev in range(8)])  98.1 us
    reduce_scatter x1, waiting for transfers between devices, shards(): lax.psum_scatter(jnp.concatenate([first, second], axis=1).astype(jnp.bflo...  93.2 us
    psum x1, waiting for transfers between devices, shards(): shard = lax.psum(shard.astype(jnp.bfloat16), 'cand').astype(jnp.float32)  35.7 us
    unnamed x72, local copies, waits for them, and re-layouts  34.1 us
    add_any x1, local copies, waits for them, and re-layouts, attend(): parts[:, :, 0]  26.1 us
    dot_general x3, matrix products, attend(): jnp.einsum('bhqk,bkhd->bqhd', probs, parts[:, :, 2], preferred_element_ty...  24.4 us
    dot_general x3, matrix products, attend(): jnp.einsum('bqhd,bkhd->bhqk', parts[:, :, 0], parts[:, :, 1], preferred_e...  23 us
    psum x1, blocking collectives, shards(): squares = lax.psum(jnp.sum(shard * shard), 'dp')  22 us
  transfers between devices with their start and end apart: 9, of which 9 were waited for; matrix products, arithmetic and copies ran while one was open for 2% of the time, Pallas kernels for 0%

profile of v1, /device:TPU:0, one launch (start us, length us, event | category | flops | bytes accessed | tf_op | source)
XLA Modules:
  0.0 496.2 jit_solution(14907487722820918671)
XLA Ops:
  10.3 16.6 %collective-permute-done = bf16[96,3072]{1,0:T(8,128)(2,1)S(1)} collective-permute-done((bf16[96,3072]{1,0:T(8,128)(2,1)}, bf16[96,3072]{1,0:T(8,128)(2,1)S(1)}, u32[]{:S(2)}, u32[]{:S(2)}) %collective-permute-start) | collective-permute-done | bytes 589856 | tf_op jit(solution)/shard_map/ppermute | solution.py:43
  27.6 17.2 %collective-permute-done.1 = bf16[96,3072]{1,0:T(8,128)(2,1)S(1)} collective-permute-done((bf16[96,3072]{1,0:T(8,128)(2,1)S(1)}, bf16[96,3072]{1,0:T(8,128)(2,1)S(1)}, u32[]{:S(2)}, u32[]{:S(2)}) %collective-permute-start.1) | collective-permute-done | bytes 589856 | tf_op jit(solution)/shard_map/ppermute | solution.py:43
  45.7 16.4 %collective-permute-done.2 = bf16[96,3072]{1,0:T(8,128)(2,1)} collective-permute-done((bf16[96,3072]{1,0:T(8,128)(2,1)S(1)}, bf16[96,3072]{1,0:T(8,128)(2,1)}, u32[]{:S(2)}, u32[]{:S(2)}) %collective-permute-start.2) | collective-permute-done | bytes 589856 | tf_op jit(solution)/shard_map/ppermute | solution.py:43
  62.9 15.0 %collective-permute-done.3 = bf16[96,3072]{1,0:T(8,128)(2,1)} collective-permute-done((bf16[96,3072]{1,0:T(8,128)(2,1)}, bf16[96,3072]{1,0:T(8,128)(2,1)}, u32[]{:S(2)}, u32[]{:S(2)}) %collective-permute-start.3) | collective-permute-done | bytes 589856 | tf_op jit(solution)/shard_map/ppermute | solution.py:43
  82.9 10.0 %collective-permute-done.4 = bf16[96,3072]{1,0:T(8,128)(2,1)} collective-permute-done((bf16[96,3072]{1,0:T(8,128)(2,1)}, bf16[96,3072]{1,0:T(8,128)(2,1)}, u32[]{:S(2)}, u32[]{:S(2)}) %collective-permute-start.4) | collective-permute-done | bytes 589856 | tf_op jit(solution)/shard_map/ppermute | solution.py:43
  92.9 3.1 multiply_convert_fusion.1
  96.0 10.8 %collective-permute-done.5 = bf16[96,3072]{1,0:T(8,128)(2,1)S(1)} collective-permute-done((bf16[96,3072]{1,0:T(8,128)(2,1)}, bf16[96,3072]{1,0:T(8,128)(2,1)S(1)}, u32[]{:S(2)}, u32[]{:S(2)}) %collective-permute-start.5) | collective-permute-done | bytes 589856 | tf_op jit(solution)/shard_map/ppermute | solution.py:43
  107.6 12.1 %collective-permute-done.6 = bf16[96,3072]{1,0:T(8,128)(2,1)S(1)} collective-permute-done((bf16[96,3072]{1,0:T(8,128)(2,1)S(1)}, bf16[96,3072]{1,0:T(8,128)(2,1)S(1)}, u32[]{:S(2)}, u32[]{:S(2)}) %collective-permute-start.6) | collective-permute-done | bytes 589856 | tf_op jit(solution)/shard_map/ppermute | solution.py:43
  126.9 3.6 copy-done.20
  130.4 10.1 %convolution_convert_fusion = bf16[2048,2304]{1,0:T(8,128)(2,1)} fusion(bf16[2048,768]{1,0:T(8,128)(2,1)S(1)} %fusion.13, bf16[1536,3072]{1,0:T(8,128)(2,1)S(1)} %constant_dynamic-update-slice_fusion, s32[]{:T(128)S(6)} %select_n.22), kind=kOutput, calls=%fused_computation.11 | convolution fusion | flops 7252475904 | bytes 16121860 | tf_op jit(solution)/shard_map/dot_general | solution.py:52
  140.5 12.7 %copy.20 = bf16[2048,2304]{0,1:T(8,128)(2,1)} copy(bf16[2048,2304]{1,0:T(8,128)(2,1)} %convolution_convert_fusion) | data formatting | bytes 18874368 | tf_op jit(solution)/shard_map/convert_element_type | solution.py:53
  153.2 10.9 %copy.45 = bf16[288,8,16,128]{3,2,1,0:T(8,128)(2,1)} copy(bf16[288,8,16,128]{3,1,2,0:T(8,128)(2,1)} %bitcast.104) | data formatting | bytes 18874368
  164.1 6.3 %fusion.57 = (bf16[16,128,1,12,64]{1,0,4,3,2:T(8,128)(2,1)}, bf16[16,128,1,12,64]{1,0,4,3,2:T(8,128)(2,1)}, bf16[16,128,1,12,64]{1,0,4,3,2:T(8,128)(2,1)S(1)}) fusion(bf16[16,128,3,12,64]{1,0,4,3,2:T(8,128)(2,1)} %bitcast.103), kind=kLoop, calls=%fused_computation.108 | loop fusion | bytes 18874368 | tf_op jit(solution)/shard_map/jvp()/slice | solution.py:30
  170.4 7.5 %fusion.5 = (f32[16,12,128]{2,1,0:T(8,128)S(1)}, f32[16,12,128,128]{2,3,1,0:T(8,128)S(1)}) fusion(f32[12,128,128]{1,2,0:T(8,128)S(1)} %copy-done.11, pred[16,128]{1,0:T(8,128)(4,1)S(1)} %iota_compare_fusion, bf16[16,128,1,12,64]{1,0,4,3,2:T(8,128)(2,1)S(1)} %get-tuple-element.15, bf16[16,128,1,12,64]{1,0,4,3,2:T(8,128)(2,1)} %get-tuple-element.14), kind=kOutput, calls=%fused_computation.13 | convolution fusion | flops 412065792 | bytes 19761152 | tf_op jit(solution)/shard_map/jvp(bqhd,bkhd->bhqk)/dot_general | solution.py:20
  178.0 3.4 fusion.37
  182.6 8.1 %convert_reduce_fusion = (f32[16,12,128]{2,1,0:T(8,128)S(1)}, pred[16,12,128,128]{2,3,1,0:T(32,128)(4,1)}, bf16[16,12,128,128]{2,3,1,0:T(8,128)(2,1)S(1)}) fusion(f32[16,12,128]{2,1,0:T(8,128)S(1)} %get-tuple-element.20, f32[16,12,128,128]{2,3,1,0:T(8,128)S(1)} %get-tuple-element.21, f32[12,128,128]{1,2,0:T(8,128)S(1)} %copy-done.11, ...), kind=kLoop, calls=%fused_computation.7 | loop fusion | flops 25141248 | bytes 23103488 | tf_op jit(solution)/shard_map/jvp()/reduce_sum | solution.py:26
  194.8 4.9 fusion.15
  200.3 5.8 %pmax.7 = f32[2]{0:T(128)S(1)} all-reduce(f32[2]{0:T(128)S(1)} %reduce_max.19), channel_id=1, replica_groups=mesh['dp'=8,'cand'=4] {'cand'}, use_global_device_ids=true, to_apply=%region_7.8 | all-reduce | flops 2 | bytes 16 | tf_op jit(solution)/shard_map/pmax | solution.py:65
  206.3 5.8 %all-reduce.3 = (f32[2]{0:T(128)S(1)}, f32[2]{0:T(128)S(1)}, f32[2]{0:T(128)S(1)}) all-reduce(f32[2]{0:T(128)S(1)} %get-tuple-element.3, f32[2]{0:T(128)S(1)} %get-tuple-element.4, f32[2]{0:T(128)S(1)} %get-tuple-element.2), channel_id=1, replica_groups=mesh['dp'=8,'cand'=4] {'cand'}, use_global_device_ids=true, to_apply=%region_11.12 | all-reduce | flops 6 | bytes 48 | tf_op jit(solution)/shard_map/psum | solution.py:66
  213.0 5.5 %convolution_convert_fusion.2 = bf16[2048,768]{1,0:T(8,128)(2,1)} fusion(bf16[2048,768]{1,0:T(8,128)(2,1)S(1)} %fusion.11, bf16[1536,3072]{1,0:T(8,128)(2,1)} %copy-done.20, s32[]{:T(128)S(6)} %select_n.22, s32[]{:T(128)S(6)} %add.82), kind=kOutput, calls=%fused_computation.41 | convolution fusion | flops 2417491968 | bytes 7471112 | tf_op jit(solution)/shard_map/dot_general | solution.py:79
  218.5 4.7 copy.27
  227.7 9.0 %convert_bitcast_fusion.2 = bf16[16,128,1,12,64]{1,4,3,0,2:T(8,128)(2,1)} fusion(bf16[16,12,128,128]{2,3,1,0:T(8,128)(2,1)} %copy-done.2, bf16[16,12,64,128]{3,0,2,1:T(8,128)(2,1)S(1)} %bitcast.108), kind=kOutput, calls=%fused_computation.50 | convolution fusion | flops 404226048 | bytes 12582912 | tf_op jit(solution)/shard_map/transpose(jvp(bhqk,bkhd->bqhd))/dot_general | solution.py:29
  236.8 12.6 %fusion.3 = (f32[16,12,128]{2,1,0:T(8,128)S(1)}, bf16[16,12,128,128]{2,3,1,0:T(8,128)(2,1)}) fusion(f32[16,12,128]{2,1,0:T(8,128)S(1)} %multiply_divide_fusion, f32[16,12,128]{2,1,0:T(8,128)S(1)} %get-tuple-element.20, f32[16,12,128,128]{2,3,1,0:T(8,128)} %copy-done, f32[12,128,128]{1,2,0:T(8,128)S(1)} %copy-done.11, ...), kind=kOutput, calls=%fused_computation.5 | convolution fusion | flops 427794432 | bytes 26249216 | tf_op jit(solution)/shard_map/transpose(jvp(bhqk,bkhd->bqhd))/dot_general | solution.py:29
  249.5 10.1 %fusion.54 = (f32[16,12,128]{2,1,0:T(8,128)S(1)}, f32[16,12,128,128]{2,3,1,0:T(8,128)}) fusion(f32[16,12,128]{2,1,0:T(8,128)S(1)} %get-tuple-element.20, f32[16,12,128,128]{2,3,1,0:T(8,128)S(1)} %bitcast.102, f32[12,128,128]{1,2,0:T(8,128)S(1)} %copy-done.11, pred[16,128]{1,0:T(8,128)(4,1)S(1)} %iota_compare_fusion, f32[16,12,128]{2,1,0:T(8,128)S(1)} %neg.9, ...), kind=kLoop, calls=%fused_computation.107 | loop fusion | flops 25141248 | bytes 32638976 | tf_op jit(solution)/shard_map/transpose(jvp())/reduce_sum | solution.py:27
  259.7 11.3 %convert_bitcast_fusion.1 = bf16[16,128,1,12,64]{1,4,3,0,2:T(8,128)(2,1)} fusion(bf16[16,128,1,12,64]{1,0,4,3,2:T(8,128)(2,1)} %get-tuple-element.14, f32[16,12,128,128]{2,3,1,0:T(8,128)} %get-tuple-element.9, pred[16,12,128,128]{2,3,1,0:T(32,128)(4,1)} %get-tuple-element.11, f32[16,12,128]{2,1,0:T(8,128)S(1)} %negate_divide_fusion, ...), kind=kOutput, calls=%fused_computation.49 | convolution fusion | flops 413663232 | bytes 22120448 | tf_op jit(solution)/shard_map/transpose(jvp(bqhd,bkhd->bhqk))/dot_general | solution.py:20
  272.5 4.2 convert_bitcast_fusion
  278.9 8.2 %pad_add_fusion = bf16[16,128,3,12,64]{1,4,3,0,2:T(8,128)(2,1)} fusion(bf16[16,128,1,12,64]{1,4,3,0,2:T(8,128)(2,1)} %convert_bitcast_fusion, bf16[16,128,1,12,64]{1,4,3,0,2:T(8,128)(2,1)} %convert_bitcast_fusion.1, bf16[16,128,1,12,64]{1,4,3,0,2:T(8,128)(2,1)} %convert_bitcast_fusion.2), kind=kLoop, calls=%fused_computation.17 | loop fusion | flops 9437184 | bytes 18874368 | tf_op jit(solution)/shard_map/transpose(jvp())/add_any | solution.py:21
  287.1 26.1 %copy.33 = bf16[16,128,3,12,64]{1,0,4,3,2:T(8,128)(2,1)} copy(bf16[16,128,3,12,64]{1,4,3,0,2:T(8,128)(2,1)} %pad_add_fusion) | data formatting | bytes 18874368 | tf_op jit(solution)/shard_map/transpose(jvp())/add_any | solution.py:21
  315.7 11.4 %fusion.22 = bf16[768,2304]{1,0:T(8,128)(2,1)S(1)} fusion(bf16[2048,768]{1,0:T(8,128)(2,1)S(1)} %bitcast.113, bf16[288,8,16,128]{3,2,1,0:T(8,128)(2,1)} %bitcast.110), kind=kOutput, calls=%fused_computation.37 | convolution fusion | flops 7249526784 | bytes 16121856 | tf_op jit(solution)/shard_map/dot_general | solution.py:83
  332.6 93.2 %reduce-scatter.2.cloned.1.call-done = bf16[96,3072]{1,0:T(8,128)(2,1)} async-done(((bf16[768,3072]{1,0:T(8,128)(2,1)}), bf16[96,3072]{1,0:T(8,128)(2,1)}) %reduce-scatter.2.cloned.1.call-update) | async-done | bytes 589840 | tf_op jit(solution)/shard_map/reduce_scatter | solution.py:85
  425.8 35.7 %all-reduce.6.cloned.1.call-done = bf16[96,3072]{1,0:T(8,128)(2,1)} async-done(((bf16[96,3072]{1,0:T(8,128)(2,1)}), bf16[96,3072]{1,0:T(8,128)(2,1)}) %all-reduce.6.cloned.1.call-update) | async-done | bytes 589840 | tf_op jit(solution)/shard_map/psum | solution.py:91
  464.0 22.0 %psum.38 = f32[]{:T(128)} all-reduce(f32[]{:T(128)} %fusion.41), channel_id=1, replica_groups=mesh['dp'=8,'cand'=4] {'dp'}, use_global_device_ids=true, to_apply=%region_19.20 | all-reduce | flops 1 | bytes 8 | tf_op jit(solution)/shard_map/psum | solution.py:92
  (113 shorter events, 46.2 us)
Async XLA Ops:
  7.2 85.8 %copy-start.5 = (bf16[2,8,128,768]{3,2,1,0:T(8,128)(2,1)S(1)}, bf16[2,8,128,768]{3,2,1,0:T(8,128)(2,1)}, u32[]{:S(2)}) copy-start(bf16[2,8,128,768]{3,2,1,0:T(8,128)(2,1)} %param.7) | copy-start | bytes 9437188
  7.2 99.6 %copy-start.22 = (f32[768]{0:T(1024)S(1)}, f32[768]{0:T(1024)}, u32[]{:S(2)}) copy-start(f32[768]{0:T(1024)} %param.9) | copy-start | bytes 9220
  7.2 418.6 %reduce-scatter.2.cloned.1.call-start = ((), (), s32[]{:S(2)}) async-start(), calls=%async_computation.1 | async-start | bytes 5308416 | tf_op jit(solution)/shard_map/reduce_scatter | solution.py:85
  7.2 19.6 %collective-permute-start = (bf16[96,3072]{1,0:T(8,128)(2,1)}, bf16[96,3072]{1,0:T(8,128)(2,1)S(1)}, u32[]{:S(2)}, u32[]{:S(2)}) collective-permute-start(bf16[96,3072]{1,0:T(8,128)(2,1)} %param.8), channel_id=1, source_target_pairs={{0,4},{4,8},{8,12},{12,16},{16,20},{20,24},{24,28},{28,0},{1,5},{5... | collective-permute-start | bytes 1769480 | tf_op jit(solution)/shard_map/ppermute | solution.py:43
  27.6 17.2 %collective-permute-start.1 = (bf16[96,3072]{1,0:T(8,128)(2,1)S(1)}, bf16[96,3072]{1,0:T(8,128)(2,1)S(1)}, u32[]{:S(2)}, u32[]{:S(2)}) collective-permute-start(bf16[96,3072]{1,0:T(8,128)(2,1)S(1)} %collective-permute-done), channel_id=1, source_target_pairs={{0,4},{4,8},{8,12},{12,16},{16,20},{20,24},{24,28},{28,0},{1,5},{5... | collective-permute-start | bytes 1769480 | tf_op jit(solution)/shard_map/ppermute | solution.py:43
  45.7 16.4 %collective-permute-start.2 = (bf16[96,3072]{1,0:T(8,128)(2,1)S(1)}, bf16[96,3072]{1,0:T(8,128)(2,1)}, u32[]{:S(2)}, u32[]{:S(2)}) collective-permute-start(bf16[96,3072]{1,0:T(8,128)(2,1)S(1)} %collective-permute-done.1), channel_id=1, source_target_pairs={{0,4},{4,8},{8,12},{12,16},{16,20},{20,24},{24,28},{28,0},{1,5},{5... | collective-permute-start | bytes 1769480 | tf_op jit(solution)/shard_map/ppermute | solution.py:43
  62.1 15.8 %collective-permute-start.3 = (bf16[96,3072]{1,0:T(8,128)(2,1)}, bf16[96,3072]{1,0:T(8,128)(2,1)}, u32[]{:S(2)}, u32[]{:S(2)}) collective-permute-start(bf16[96,3072]{1,0:T(8,128)(2,1)} %collective-permute-done.2), channel_id=1, source_target_pairs={{0,4},{4,8},{8,12},{12,16},{16,20},{20,24},{24,28},{28,0},{1,5},{5... | collective-permute-start | bytes 1769480 | tf_op jit(solution)/shard_map/ppermute | solution.py:43
  77.9 14.9 %collective-permute-start.4 = (bf16[96,3072]{1,0:T(8,128)(2,1)}, bf16[96,3072]{1,0:T(8,128)(2,1)}, u32[]{:S(2)}, u32[]{:S(2)}) collective-permute-start(bf16[96,3072]{1,0:T(8,128)(2,1)} %collective-permute-done.3), channel_id=1, source_target_pairs={{0,4},{4,8},{8,12},{12,16},{16,20},{20,24},{24,28},{28,0},{1,5},{5... | collective-permute-start | bytes 1769480 | tf_op jit(solution)/shard_map/ppermute | solution.py:43
  92.8 14.0 %collective-permute-start.5 = (bf16[96,3072]{1,0:T(8,128)(2,1)}, bf16[96,3072]{1,0:T(8,128)(2,1)S(1)}, u32[]{:S(2)}, u32[]{:S(2)}) collective-permute-start(bf16[96,3072]{1,0:T(8,128)(2,1)} %collective-permute-done.4), channel_id=1, source_target_pairs={{0,4},{4,8},{8,12},{12,16},{16,20},{20,24},{24,28},{28,0},{1,5},{5... | collective-permute-start | bytes 1769480 | tf_op jit(solution)/shard_map/ppermute | solution.py:43
  96.0 27.1 %copy-start.19 = (bf16[96,3072]{1,0:T(8,128)(2,1)S(1)}, bf16[96,3072]{1,0:T(8,128)(2,1)}, u32[]{:S(2)}) copy-start(bf16[96,3072]{1,0:T(8,128)(2,1)} %copy-done.18) | copy-start | bytes 1769476
  106.8 12.9 %collective-permute-start.6 = (bf16[96,3072]{1,0:T(8,128)(2,1)S(1)}, bf16[96,3072]{1,0:T(8,128)(2,1)S(1)}, u32[]{:S(2)}, u32[]{:S(2)}) collective-permute-start(bf16[96,3072]{1,0:T(8,128)(2,1)S(1)} %collective-permute-done.5), channel_id=1, source_target_pairs={{0,4},{4,8},{8,12},{12,16},{16,20},{20,24},{24,28},{28,0},{1,5},{5... | collective-permute-start | bytes 1769480 | tf_op jit(solution)/shard_map/ppermute | solution.py:43
  106.8 16.4 %copy-start.17 = (bf16[96,3072]{1,0:T(8,128)(2,1)S(1)}, bf16[96,3072]{1,0:T(8,128)(2,1)}, u32[]{:S(2)}) copy-start(bf16[96,3072]{1,0:T(8,128)(2,1)} %copy-done.16) | copy-start | bytes 1769476
  106.8 16.4 %copy-start.15 = (bf16[96,3072]{1,0:T(8,128)(2,1)S(1)}, bf16[96,3072]{1,0:T(8,128)(2,1)}, u32[]{:S(2)}) copy-start(bf16[96,3072]{1,0:T(8,128)(2,1)} %param.8) | copy-start | bytes 1769476
  126.9 3.6 copy-start.20
  164.1 6.3 %copy-start.11 = (f32[12,128,128]{1,2,0:T(8,128)S(1)}, f32[12,128,128]{1,2,0:T(8,128)}, u32[]{:S(2)}) copy-start(f32[12,128,128]{1,2,0:T(8,128)} %copy.24) | copy-start | bytes 2359300
  170.4 7.6 %copy-start.3 = (bf16[16,128,1,12,64]{1,0,4,3,2:T(8,128)(2,1)}, bf16[16,128,1,12,64]{1,0,4,3,2:T(8,128)(2,1)S(1)}, u32[]{:S(2)}) copy-start(bf16[16,128,1,12,64]{1,0,4,3,2:T(8,128)(2,1)S(1)} %get-tuple-element.15) | copy-start | bytes 9437188
  178.0 4.6 copy-start
  182.6 8.1 %copy-start.8 = (bf16[16,128,1,12,64]{1,0,4,3,2:T(8,128)(2,1)S(1)}, bf16[16,128,1,12,64]{1,0,4,3,2:T(8,128)(2,1)}, u32[]{:S(2)}) copy-start(bf16[16,128,1,12,64]{1,0,4,3,2:T(8,128)(2,1)} %get-tuple-element.13) | copy-start | bytes 9437188
  190.7 3.2 copy-start.2
  190.7 4.2 copy-start.6
  193.9 5.9 %copy-start.9 = (bf16[16,12,64,128]{3,2,1,0:T(8,128)(2,1)}, bf16[16,12,64,128]{3,2,1,0:T(8,128)(2,1)S(1)}, u32[]{:S(2)}) copy-start(bf16[16,12,64,128]{3,2,1,0:T(8,128)(2,1)S(1)} %fusion.36) | copy-start | bytes 9437188
  194.8 5.1 %copy-start.21 = (f32[768]{0:T(1024)S(1)}, f32[768]{0:T(1024)}, u32[]{:S(2)}) copy-start(f32[768]{0:T(1024)} %param.11) | copy-start | bytes 9220
  194.8 11.3 %copy-start.23 = (s32[2,8]{1,0:T(2,128)S(1)}, s32[2,8]{1,0:T(2,128)}, u32[]{:S(2)}) copy-start(s32[2,8]{1,0:T(2,128)} %param.13) | copy-start | bytes 196
  227.7 21.7 %slice-start = ((s8[12582912]{0:T(1024)(128)(4,1)}), s8[4194304]{0:T(1024)(128)(4,1)S(1)}, s32[]{:S(2)}) async-start(s8[12582912]{0:T(1024)(128)(4,1)} %bitcast.101), calls=%async_computation.3 | async-start | bytes 8388608
  236.8 12.7 %slice-start.1 = ((s8[12582912]{0:T(1024)(128)(4,1)}), s8[4194304]{0:T(1024)(128)(4,1)S(1)}, s32[]{:S(2)}) async-start(s8[12582912]{0:T(1024)(128)(4,1)} %bitcast.101), calls=%async_computation.4 | async-start | bytes 8388608
  236.8 12.7 %slice-start.2 = ((s8[12582912]{0:T(1024)(128)(4,1)}), s8[4194304]{0:T(1024)(128)(4,1)S(1)}, s32[]{:S(2)}) async-start(s8[12582912]{0:T(1024)(128)(4,1)} %bitcast.101), calls=%async_computation.5 | async-start | bytes 8388608
  259.6 11.3 %copy-start.1 = (f32[16,12,128,128]{2,3,1,0:T(8,128)S(1)}, f32[16,12,128,128]{2,3,1,0:T(8,128)}, u32[]{:S(2)}) copy-start(f32[16,12,128,128]{2,3,1,0:T(8,128)} %get-tuple-element.9) | copy-start | bytes 37748740
  259.7 12.0 %copy-start.4 = (bf16[16,128,1,12,64]{1,0,4,3,2:T(8,128)(2,1)S(1)}, bf16[16,128,1,12,64]{1,0,4,3,2:T(8,128)(2,1)}, u32[]{:S(2)}) copy-start(bf16[16,128,1,12,64]{1,0,4,3,2:T(8,128)(2,1)} %copy-done.3) | copy-start | bytes 9437188
  259.7 12.9 %copy-start.7 = (pred[16,12,128,128]{2,3,1,0:T(32,128)(4,1)S(1)}, pred[16,12,128,128]{2,3,1,0:T(32,128)(4,1)}, u32[]{:S(2)}) copy-start(pred[16,12,128,128]{2,3,1,0:T(32,128)(4,1)} %get-tuple-element.11) | copy-start | bytes 9437188
  287.1 26.2 %copy-start.10 = (bf16[16,12,64,128]{3,2,1,0:T(8,128)(2,1)S(1)}, bf16[16,12,64,128]{3,2,1,0:T(8,128)(2,1)}, u32[]{:S(2)}) copy-start(bf16[16,12,64,128]{3,2,1,0:T(8,128)(2,1)} %copy-done.9) | copy-start | bytes 9437188
  315.7 11.4 %copy-start.13 = (bf16[16,128,768]{2,1,0:T(8,128)(2,1)S(1)}, bf16[16,128,768]{2,1,0:T(8,128)(2,1)}, u32[]{:S(2)}) copy-start(bf16[16,128,768]{2,1,0:T(8,128)(2,1)} %multiply_convert_fusion) | copy-start | bytes 9437188
  332.5 129.0 %all-reduce.6.cloned.1.call-start = ((), (), s32[]{:S(2)}) async-start(), calls=%async_computation.2 | async-start | bytes 1179648 | tf_op jit(solution)/shard_map/psum | solution.py:91
  (4 other events, 5.7 us)
Sparse Core Ops, SparseCore 0:
  332.6 93.1 reduce-scatter.1
  428.1 33.3 all-reduce.5
